TPU v7x, 32 devices: a whole 2x2x4 slice. The times are simulated.
32 devices in a mesh: seq: 8 (over z, y), shard: 4 (over x, core).
Axes of the slice: x: 2, y: 2, z: 4, core: 2. Of those that a mesh axis runs over, the one named last changes fastest.
Arguments:
- tokens: bfloat16 [8, 4096, 768], P('shard', 'seq'), may hold values from -6 to 6
- segments: int32 [8, 4096], P('shard'), may hold values from 0 to 20, as said below
- positions: int32 [8, 4096], P('shard', 'seq'), may hold values from 0 to 1999, as said below
- cotangent: bfloat16 [8, 4096, 768], P('shard', 'seq'), may hold values from -6 to 6
- w_qkv: bfloat16 [768, 2304], P('shard'), may hold values from -0.21875 to 0.21875
- w_out: bfloat16 [768, 768], P('shard'), may hold values from -3 to 3
- w_gate: bfloat16 [768, 3072], P('shard'), may hold values from -0.21875 to 0.21875
- w_up: bfloat16 [768, 3072], P('shard'), may hold values from -0.21875 to 0.21875
- w_down: bfloat16 [3072, 768], P('shard'), may hold values from -0.109375 to 0.109375
- ln1_gain: bfloat16 [768], P('shard'), may hold values from 0.099609375 to 1.8984375
- ln1_bias: bfloat16 [768], P('shard'), may hold values from -3 to 3
- ln2_gain: bfloat16 [768], P('shard'), may hold values from 0.099609375 to 1.8984375
- ln2_bias: bfloat16 [768], P('shard'), may hold values from -3 to 3
Outputs:
- output: bfloat16 [8, 4096, 768], P('shard', 'seq')
- input_grad: bfloat16 [8, 4096, 768], P('shard', 'seq')
- grad_w_qkv: float32 [768, 2304], P('shard')
- grad_w_out: float32 [768, 768], P('shard')
- grad_w_gate: float32 [768, 3072], P('shard')
- grad_w_up: float32 [768, 3072], P('shard')
- grad_w_down: float32 [3072, 768], P('shard')
- grad_ln1_gain: float32 [768], P('shard')
- grad_ln1_bias: float32 [768], P('shard')
- grad_ln2_gain: float32 [768], P('shard')
- grad_ln2_bias: float32 [768], P('shard')
Inputs may be any that keep to these rules, and one draw needn't show every extreme that they name: segments[s, t] numbers the documents of sequence s in order from 0 and never falls along t; every document has 200 to 2000 tokens, except that the end of the sequence may cut the last one short. positions[s, t] counts the earlier tokens of the same document of sequence s.
All inputs are finite; a program needn't handle non-finite values.
Results may differ from a plain program's by a relative error of at most 0.025.
Values may be sent and summed in bfloat16 or wider, within the bound.
A program may use at most 256 MiB of HBM per device.

v0:
```python
import math
import jax
import jax.numpy as jnp
from jax import lax
from jax.sharding import PartitionSpec as P

HEADS = 12
HD = 64
EPS = 1e-05
ROPE_BASE = 1000.0


def rope_tables(pos_block):
    half_dim = HD // 2
    freqs = jnp.exp(jnp.arange(half_dim, dtype=jnp.float32) * (-math.log(ROPE_BASE) / half_dim))
    angle = pos_block.astype(jnp.float32)[..., None] * freqs
    return (jnp.cos(angle)[:, :, None, :], jnp.sin(angle)[:, :, None, :])


def rotate(heads, cos_b, sin_b):
    half_dim = heads.shape[-1] // 2
    first = heads[..., :half_dim]
    second = heads[..., half_dim:]
    return jnp.concatenate(
        [first * cos_b - second * sin_b, second * cos_b + first * sin_b], axis=-1
    )


def rotate_back(grads, cos_b, sin_b):
    half_dim = grads.shape[-1] // 2
    first = grads[..., :half_dim]
    second = grads[..., half_dim:]
    return jnp.concatenate(
        [first * cos_b + second * sin_b, second * cos_b - first * sin_b], axis=-1
    )


def norm_fwd(values, gain, bias):
    mean_val = jnp.mean(values, axis=-1, keepdims=True)
    centered = values - mean_val
    variance = jnp.mean(centered * centered, axis=-1, keepdims=True)
    inverse = lax.rsqrt(variance + EPS)
    normed = centered * inverse
    return (normed * gain + bias, normed, inverse)


def norm_back(grad_in, normed, inverse, gain):
    scaled = grad_in * gain
    return inverse * (
        scaled
        - jnp.mean(scaled, axis=-1, keepdims=True)
        - normed * jnp.mean(scaled * normed, axis=-1, keepdims=True)
    )


def head_split(block_rows, seq_count, row_count):
    return block_rows.reshape(seq_count, row_count, HEADS, HD)


def attend(q_heads, q_seg, k_full, v_full, seg_all, block, score_scale):
    seq_count, row_count = (q_heads.shape[0], q_heads.shape[1])
    block_count = k_full.shape[1] // block

    def attend_step(carry, index):
        row_total, value_sum = carry
        start = index * block
        k_part = head_split(lax.dynamic_slice_in_dim(k_full, start, block, 1), seq_count, block)
        v_part = head_split(lax.dynamic_slice_in_dim(v_full, start, block, 1), seq_count, block)
        seg_part = lax.dynamic_slice_in_dim(seg_all, start, block, 1)
        raw = (
            jnp.einsum("sqhd,skhd->shqk", q_heads, k_part, preferred_element_type=jnp.float32)
            * score_scale
        )
        same_doc = q_seg[:, None, :, None] == seg_part[:, None, None, :]
        expo = jnp.where(same_doc, jnp.exp(raw), 0.0)
        row_total = row_total + jnp.sum(expo, axis=-1)
        value_sum = value_sum + jnp.einsum(
            "shqk,skhd->sqhd", expo.astype(jnp.bfloat16), v_part, preferred_element_type=jnp.float32
        )
        return ((row_total, value_sum), None)

    start_carry = (
        jnp.zeros((seq_count, HEADS, row_count), jnp.float32),
        jnp.zeros((seq_count, row_count, HEADS, HD), jnp.float32),
    )
    final, unused = lax.scan(attend_step, start_carry, jnp.arange(block_count, dtype=jnp.int32))
    return final


def back_keys(q_heads, g_heads, delta, q_seg, k_full, v_full, seg_all, block, score_scale):
    seq_count, row_count = (q_heads.shape[0], q_heads.shape[1])
    full_len = k_full.shape[1]
    block_count = full_len // block

    def back_step(carry, index):
        start = index * block
        k_part = head_split(lax.dynamic_slice_in_dim(k_full, start, block, 1), seq_count, block)
        v_part = head_split(lax.dynamic_slice_in_dim(v_full, start, block, 1), seq_count, block)
        seg_part = lax.dynamic_slice_in_dim(seg_all, start, block, 1)
        raw = (
            jnp.einsum("sqhd,skhd->shqk", q_heads, k_part, preferred_element_type=jnp.float32)
            * score_scale
        )
        same_doc = q_seg[:, None, :, None] == seg_part[:, None, None, :]
        expo = jnp.where(same_doc, jnp.exp(raw), 0.0)
        prob_grad = jnp.einsum(
            "sqhd,skhd->shqk", g_heads, v_part, preferred_element_type=jnp.float32
        )
        d_score = (expo * (prob_grad - delta[..., None])).astype(jnp.bfloat16)
        q_grad = carry[0] + jnp.einsum(
            "shqk,skhd->sqhd", d_score, k_part, preferred_element_type=jnp.float32
        )
        k_grad = (
            jnp.einsum("shqk,sqhd->skhd", d_score, q_heads, preferred_element_type=jnp.float32)
            * score_scale
        )
        v_grad = jnp.einsum(
            "shqk,sqhd->skhd",
            expo.astype(jnp.bfloat16),
            g_heads,
            preferred_element_type=jnp.float32,
        )
        k_store = lax.dynamic_update_slice_in_dim(
            carry[1], k_grad.reshape(seq_count, block, HEADS * HD), start, 1
        )
        v_store = lax.dynamic_update_slice_in_dim(
            carry[2], v_grad.reshape(seq_count, block, HEADS * HD), start, 1
        )
        return ((q_grad, k_store, v_store), None)

    q_zero = jnp.zeros((seq_count, row_count, HEADS, HD), jnp.float32)
    kv_zero = jnp.zeros((seq_count, full_len, HEADS * HD), jnp.float32)
    start_carry = (q_zero, kv_zero, kv_zero)
    final, unused = lax.scan(back_step, start_carry, jnp.arange(block_count, dtype=jnp.int32))
    return (final[0] * score_scale,) + tuple(final[1:])


def local(
    tokens,
    segments,
    positions,
    cotangent,
    w_qkv,
    w_out,
    w_gate,
    w_up,
    w_down,
    ln1_gain,
    ln1_bias,
    ln2_gain,
    ln2_bias,
):
    seq_count, row_count, model_width = tokens.shape
    score_scale = HD ** (-0.5)
    q_seg = lax.dynamic_slice_in_dim(segments, lax.axis_index("seq") * row_count, row_count, 1)
    gathered = (
        lax.all_gather(w_qkv, "shard", axis=0, tiled=True),
        lax.all_gather(w_out, "shard", axis=0, tiled=True),
        lax.all_gather(w_gate, "shard", axis=0, tiled=True),
        lax.all_gather(w_up, "shard", axis=0, tiled=True),
        lax.all_gather(w_down, "shard", axis=0, tiled=True),
        lax.all_gather(ln1_gain, "shard", axis=0, tiled=True),
        lax.all_gather(ln1_bias, "shard", axis=0, tiled=True),
        lax.all_gather(ln2_gain, "shard", axis=0, tiled=True),
        lax.all_gather(ln2_bias, "shard", axis=0, tiled=True),
    )
    full_qkv, full_out, full_gate, full_up, full_down, gain_one, bias_one, gain_two, bias_two = (
        gathered
    )
    cos_b, sin_b = rope_tables(positions)
    qkv_all = jnp.einsum("scd,de->sce", tokens, full_qkv, preferred_element_type=jnp.float32)
    q_heads = rotate(
        head_split(qkv_all[..., :model_width], seq_count, row_count), cos_b, sin_b
    ).astype(jnp.bfloat16)
    k_heads = rotate(
        head_split(qkv_all[..., model_width : 2 * model_width], seq_count, row_count), cos_b, sin_b
    ).astype(jnp.bfloat16)
    v_heads = head_split(qkv_all[..., 2 * model_width :], seq_count, row_count).astype(jnp.bfloat16)
    k_local = k_heads.reshape(seq_count, row_count, model_width)
    v_local = v_heads.reshape(seq_count, row_count, model_width)
    k_full, v_full = (
        lax.all_gather(k_local, "seq", axis=1, tiled=True),
        lax.all_gather(v_local, "seq", axis=1, tiled=True),
    )
    row_total, value_sum = attend(q_heads, q_seg, k_full, v_full, segments, row_count, score_scale)
    denom = jnp.transpose(row_total, (0, 2, 1))[..., None]
    attn_out = value_sum / denom
    joined = attn_out.reshape(seq_count, row_count, model_width).astype(jnp.bfloat16)
    tokens_f = tokens.astype(jnp.float32)
    h_one = tokens_f + jnp.einsum(
        "sci,io->sco", joined, full_out, preferred_element_type=jnp.float32
    )
    x_one, normed_one, inverse_one = norm_fwd(
        h_one, gain_one.astype(jnp.float32), bias_one.astype(jnp.float32)
    )
    x_low = x_one.astype(jnp.bfloat16)
    gate_pre = jnp.einsum("scd,df->scf", x_low, full_gate, preferred_element_type=jnp.float32)
    up_pre = jnp.einsum("scd,df->scf", x_low, full_up, preferred_element_type=jnp.float32)
    sigma = jax.nn.sigmoid(gate_pre)
    smooth = gate_pre * sigma
    hidden = (smooth * up_pre).astype(jnp.bfloat16)
    h_two = x_one + jnp.einsum("scf,fd->scd", hidden, full_down, preferred_element_type=jnp.float32)
    result, normed_two, inverse_two = norm_fwd(
        h_two, gain_two.astype(jnp.float32), bias_two.astype(jnp.float32)
    )
    output = result.astype(jnp.bfloat16)
    regathered = (
        lax.all_gather(w_qkv, "shard", axis=0, tiled=True),
        lax.all_gather(w_out, "shard", axis=0, tiled=True),
        lax.all_gather(w_gate, "shard", axis=0, tiled=True),
        lax.all_gather(w_up, "shard", axis=0, tiled=True),
        lax.all_gather(w_down, "shard", axis=0, tiled=True),
        lax.all_gather(ln1_gain, "shard", axis=0, tiled=True),
        lax.all_gather(ln2_gain, "shard", axis=0, tiled=True),
    )
    back_qkv, back_out, back_gate, back_up, back_down, back_gain_one, back_gain_two = regathered
    back_k, back_v = (
        lax.all_gather(k_local, "seq", axis=1, tiled=True),
        lax.all_gather(v_local, "seq", axis=1, tiled=True),
    )
    cot_f = cotangent.astype(jnp.float32)
    grad_gain_two = jnp.sum(cot_f * normed_two, axis=(0, 1))
    grad_bias_two = jnp.sum(cot_f, axis=(0, 1))
    dh_two = norm_back(cot_f, normed_two, inverse_two, back_gain_two.astype(jnp.float32))
    dm_low = dh_two.astype(jnp.bfloat16)
    grad_down = jnp.einsum("scf,scd->fd", hidden, dm_low, preferred_element_type=jnp.float32)
    d_hidden = jnp.einsum("scd,fd->scf", dm_low, back_down, preferred_element_type=jnp.float32)
    d_up = (d_hidden * smooth).astype(jnp.bfloat16)
    d_gate = (d_hidden * up_pre * sigma * (1.0 + gate_pre * (1.0 - sigma))).astype(jnp.bfloat16)
    grad_gate = jnp.einsum("scd,scf->df", x_low, d_gate, preferred_element_type=jnp.float32)
    grad_up = jnp.einsum("scd,scf->df", x_low, d_up, preferred_element_type=jnp.float32)
    dx_one = (
        dh_two
        + jnp.einsum("scf,df->scd", d_gate, back_gate, preferred_element_type=jnp.float32)
        + jnp.einsum("scf,df->scd", d_up, back_up, preferred_element_type=jnp.float32)
    )
    grad_gain_one = jnp.sum(dx_one * normed_one, axis=(0, 1))
    grad_bias_one = jnp.sum(dx_one, axis=(0, 1))
    dh_one = norm_back(dx_one, normed_one, inverse_one, back_gain_one.astype(jnp.float32))
    d_attn = dh_one.astype(jnp.bfloat16)
    grad_out = jnp.einsum("sci,sco->io", joined, d_attn, preferred_element_type=jnp.float32)
    d_joined = jnp.einsum(
        "sco,io->sci", d_attn, back_out, preferred_element_type=jnp.float32
    ).astype(jnp.bfloat16)
    d_heads = head_split(d_joined, seq_count, row_count).astype(jnp.float32)
    g_heads = (d_heads / denom).astype(jnp.bfloat16)
    delta = jnp.transpose(jnp.sum(d_heads * attn_out, axis=-1) / denom[..., 0], (0, 2, 1))
    q_grad, k_all, v_all = back_keys(
        q_heads, g_heads, delta, q_seg, back_k, back_v, segments, row_count, score_scale
    )
    k_sum, v_sum = (
        lax.psum_scatter(k_all.astype(jnp.bfloat16), "seq", scatter_dimension=1, tiled=True).astype(
            jnp.float32
        ),
        lax.psum_scatter(v_all.astype(jnp.bfloat16), "seq", scatter_dimension=1, tiled=True).astype(
            jnp.float32
        ),
    )
    k_grad = head_split(k_sum, seq_count, row_count)
    v_grad = head_split(v_sum, seq_count, row_count)
    q_back = rotate_back(q_grad, cos_b, sin_b).reshape(seq_count, row_count, model_width)
    k_back = rotate_back(k_grad, cos_b, sin_b).reshape(seq_count, row_count, model_width)
    d_qkv = jnp.concatenate(
        [q_back, k_back, v_grad.reshape(seq_count, row_count, model_width)], axis=-1
    ).astype(jnp.bfloat16)
    grad_qkv = jnp.einsum("scd,sce->de", tokens, d_qkv, preferred_element_type=jnp.float32)
    d_tokens = dh_one + jnp.einsum(
        "sce,de->scd", d_qkv, back_qkv, preferred_element_type=jnp.float32
    )
    input_grad = d_tokens.astype(jnp.bfloat16)
    owned = (
        lax.psum_scatter(
            grad_qkv.astype(jnp.bfloat16), "shard", scatter_dimension=0, tiled=True
        ).astype(jnp.float32),
        lax.psum_scatter(
            grad_out.astype(jnp.bfloat16), "shard", scatter_dimension=0, tiled=True
        ).astype(jnp.float32),
        lax.psum_scatter(
            grad_gate.astype(jnp.bfloat16), "shard", scatter_dimension=0, tiled=True
        ).astype(jnp.float32),
        lax.psum_scatter(
            grad_up.astype(jnp.bfloat16), "shard", scatter_dimension=0, tiled=True
        ).astype(jnp.float32),
        lax.psum_scatter(
            grad_down.astype(jnp.bfloat16), "shard", scatter_dimension=0, tiled=True
        ).astype(jnp.float32),
        lax.psum_scatter(
            grad_gain_one.astype(jnp.bfloat16), "shard", scatter_dimension=0, tiled=True
        ).astype(jnp.float32),
        lax.psum_scatter(
            grad_bias_one.astype(jnp.bfloat16), "shard", scatter_dimension=0, tiled=True
        ).astype(jnp.float32),
        lax.psum_scatter(
            grad_gain_two.astype(jnp.bfloat16), "shard", scatter_dimension=0, tiled=True
        ).astype(jnp.float32),
        lax.psum_scatter(
            grad_bias_two.astype(jnp.bfloat16), "shard", scatter_dimension=0, tiled=True
        ).astype(jnp.float32),
    )
    summed = (
        lax.psum(owned[0].astype(jnp.bfloat16), "seq").astype(jnp.float32),
        lax.psum(owned[1].astype(jnp.bfloat16), "seq").astype(jnp.float32),
        lax.psum(owned[2].astype(jnp.bfloat16), "seq").astype(jnp.float32),
        lax.psum(owned[3].astype(jnp.bfloat16), "seq").astype(jnp.float32),
        lax.psum(owned[4].astype(jnp.bfloat16), "seq").astype(jnp.float32),
        lax.psum(owned[5].astype(jnp.bfloat16), "seq").astype(jnp.float32),
        lax.psum(owned[6].astype(jnp.bfloat16), "seq").astype(jnp.float32),
        lax.psum(owned[7].astype(jnp.bfloat16), "seq").astype(jnp.float32),
        lax.psum(owned[8].astype(jnp.bfloat16), "seq").astype(jnp.float32),
    )
    return (
        output,
        input_grad,
        summed[0],
        summed[1],
        summed[2],
        summed[3],
        summed[4],
        summed[5],
        summed[6],
        summed[7],
        summed[8],
    )


def solution(mesh):
    in_specs = (
        P("shard", "seq", None),
        P("shard", None),
        P("shard", "seq"),
        P("shard", "seq", None),
        P("shard", None),
        P("shard", None),
        P("shard", None),
        P("shard", None),
        P("shard", None),
        P("shard"),
        P("shard"),
        P("shard"),
        P("shard"),
    )
    out_specs = (
        P("shard", "seq", None),
        P("shard", "seq", None),
        P("shard", None),
        P("shard", None),
        P("shard", None),
        P("shard", None),
        P("shard", None),
        P("shard"),
        P("shard"),
        P("shard"),
        P("shard"),
    )
    return jax.shard_map(local, mesh=mesh, in_specs=in_specs, out_specs=out_specs, check_vma=False)
```

profile of v0, /device:TPU:0, one launch (start us, length us, event | category | flops | bytes accessed | tf_op | source)
XLA Modules:
  0.0 2137.3 jit_solution(6114114731520905912)
XLA Ops:
  8.0 35.1 %all-gather.8.cloned.1.call-done = bf16[768,2304]{1,0:T(8,128)(2,1)} async-done(((bf16[192,2304]{1,0:T(8,128)(2,1)}), bf16[768,2304]{1,0:T(8,128)(2,1)}) %all-gather.8.cloned.1.call-update) | async-done | bytes 3538960 | tf_op jit(solution)/shard_map/all_gather | solution.py:157
  86.1 144.4 %all-gather.12.cloned.1.call-done = bf16[2,4096,768]{2,1,0:T(8,128)(2,1)} async-done(((bf16[2,512,768]{2,1,0:T(8,128)(2,1)}), bf16[2,4096,768]{2,1,0:T(8,128)(2,1)}) %all-gather.12.cloned.1.call-update) | async-done | bytes 12582928 | tf_op jit(solution)/shard_map/all_gather | solution.py:183
  230.5 16.2 copy.69
  246.7 160.8 %all-gather.10.cloned.1.call-done = bf16[2,4096,768]{1,2,0:T(8,128)(2,1)} async-done(((bf16[2,512,768]{1,2,0:T(8,128)(2,1)}), bf16[2,4096,768]{1,2,0:T(8,128)(2,1)}) %all-gather.10.cloned.1.call-update) | async-done | bytes 12582928 | tf_op jit(solution)/shard_map/all_gather | solution.py:182
  407.5 236.3 %while.28 = (s32[]{:T(128)}, f32[2,12,512]{2,1,0:T(8,128)S(1)}, f32[2,512,12,64]{1,3,2,0:T(8,128)}, s32[2,512]{1,0:T(2,128)S(1)}, s32[8]{0:T(128)S(1)}, /*index=...) while((s32[]{:T(128)}, f32[2,12,512]{2,1,0:T(8,128)S(1)}, ...), condition=%wide.region_2.3_spmd.clone, body=%wide.region_0.2_spmd.clone.sunk | while | flops 1650470912 | bytes 71516400 | solution.py:86
  512.0 14.1 bitcast_add_fusion.4
  693.0 18.8 multiply_convert_fusion.1
  757.3 534.2 %while.29 = (s32[]{:T(128)}, f32[2,512,12,64]{1,3,2,0:T(8,128)}, bf16[2,4096,768]{1,2,0:T(8,128)(2,1)}, bf16[2,4096,768]{2,1,0:T(8,128)(2,1)}, s32[8]{0:T(128)S(...) while((s32[]{:T(128)}, f32[2,512,12,64]{1,3,2,0:T(8,128)}, ...), condition=%wide.region_13.14_spmd.clone, body=%wide.region_12.13_spmd.clone.sunk | while | flops 4080533504 | bytes 159449392 | solution.py:134
  774.2 15.9 fusion.129
  840.1 15.9 fusion.129
  906.9 15.9 fusion.129
  973.7 15.9 fusion.129
  1040.7 15.9 fusion.129
  1107.4 15.9 fusion.129
  1174.3 15.9 fusion.129
  1241.1 15.9 fusion.129
  1295.6 203.2 %reduce-scatter.10.cloned.1.call-done = bf16[2,512,768]{1,2,0:T(8,128)(2,1)} async-done(((bf16[2,4096,768]{1,2,0:T(8,128)(2,1)}), bf16[2,512,768]{1,2,0:T(8,128)(2,1)}) %reduce-scatter.10.cloned.1.call-update) | async-done | bytes 1572880 | tf_op jit(solution)/shard_map/reduce_scatter | solution.py:252
  1506.2 202.7 %reduce-scatter.12.cloned.1.call-done = bf16[2,512,768]{2,1,0:T(8,128)(2,1)} async-done(((bf16[2,4096,768]{2,1,0:T(8,128)(2,1)}), bf16[2,512,768]{2,1,0:T(8,128)(2,1)}) %reduce-scatter.12.cloned.1.call-update) | async-done | bytes 1572880 | tf_op jit(solution)/shard_map/reduce_scatter | solution.py:255
  1761.6 26.4 %reduce-scatter.14.cloned.1.call-done = bf16[192,768]{1,0:T(8,128)(2,1)} async-done(((bf16[768,768]{1,0:T(8,128)(2,1)}), bf16[192,768]{1,0:T(8,128)(2,1)}) %reduce-scatter.14.cloned.1.call-update) | async-done | bytes 294928 | tf_op jit(solution)/shard_map/reduce_scatter | solution.py:275
  1788.1 50.4 %reduce-scatter.16.cloned.1.call-done = bf16[192,3072]{1,0:T(8,128)(2,1)} async-done(((bf16[768,3072]{1,0:T(8,128)(2,1)}), bf16[192,3072]{1,0:T(8,128)(2,1)}) %reduce-scatter.16.cloned.1.call-update) | async-done | bytes 1179664 | tf_op jit(solution)/shard_map/reduce_scatter | solution.py:278
  1838.5 50.5 %reduce-scatter.18.cloned.1.call-done = bf16[192,3072]{1,0:T(8,128)(2,1)} async-done(((bf16[768,3072]{1,0:T(8,128)(2,1)}), bf16[192,3072]{1,0:T(8,128)(2,1)}) %reduce-scatter.18.cloned.1.call-update) | async-done | bytes 1179664 | tf_op jit(solution)/shard_map/reduce_scatter | solution.py:281
  1889.0 50.4 %reduce-scatter.20.cloned.1.call-done = bf16[768,768]{1,0:T(8,128)(2,1)} async-done(((bf16[3072,768]{1,0:T(8,128)(2,1)}), bf16[768,768]{1,0:T(8,128)(2,1)}) %reduce-scatter.20.cloned.1.call-update) | async-done | bytes 1179664 | tf_op jit(solution)/shard_map/reduce_scatter | solution.py:284
  1952.7 22.7 %all-reduce.8 = (bf16[192]{0:T(256)(128)(2,1)S(1)}, bf16[192]{0:T(256)(128)(2,1)S(1)}, bf16[192]{0:T(256)(128)(2,1)S(1)}, bf16[192]{0:T(256)(128)(2,1)S(1)}) all-reduce(bf16[192]{0:T(256)(128)(2,1)S(1)} %dynamic-slice.5, bf16[192]{0:T(256)(128)(2,1)S(1)} %dynamic-slice.7, ...), channel_id=1, replica_groups=mesh['seq'=8,'shard'=4] {'seq'}, use_global_device_ids=true, to_apply=%region_28.29 | all-reduce | flops 768 | bytes 3072 | tf_op jit(solution)/shard_map/psum | solution.py:306
  1987.4 134.7 %all-reduce.14.cloned.1.call-done = (bf16[192,2304]{0,1:T(8,128)(2,1)}, bf16[192,768]{1,0:T(8,128)(2,1)}, bf16[192,3072]{1,0:T(8,128)(2,1)}, bf16[192,3072]{1,0:T(8,128)(2,1)}, bf16[768,768]{1,0:T(8,128)(2,1)}) async-done(((bf16[192,2304]{0,1:T(8,128)(2,1)}, bf16[192,768]{1,0:T(8,128)(2,1)}, bf16[192,3072]{1,0:T(8,128)(2,1)}, bf16[192,3072]{1,0:T(8,128)(2,1)}, bf16[768,768]{1,0:T(8,128)(2,1)}), ...) | async-done | bytes 4718608 | tf_op jit(solution)/shard_map/psum | solution.py:301
  (412 shorter events, 852.2 us)
Async XLA Ops:
  7.2 35.9 %all-gather.8.cloned.1.call-start = ((), (), s32[]{:S(2)}) async-start(), calls=%async_computation.7 | async-start | bytes 4423680 | tf_op jit(solution)/shard_map/all_gather | solution.py:157
  7.9 222.6 %all-gather.12.cloned.1.call-start = ((), (), s32[]{:S(2)}) async-start(), calls=%async_computation.9 | async-start | bytes 14155776 | tf_op jit(solution)/shard_map/all_gather | solution.py:183
  54.2 353.2 %all-gather.10.cloned.1.call-start = ((), (), s32[]{:S(2)}) async-start(), calls=%async_computation.8 | async-start | bytes 14155776 | tf_op jit(solution)/shard_map/all_gather | solution.py:182
  73.3 573.5 %all-gather.14.cloned.1.call-start = ((), (), s32[]{:S(2)}) async-start(), calls=%async_computation.10 | async-start | bytes 1474560 | tf_op jit(solution)/shard_map/all_gather | solution.py:158
  73.9 579.0 %all-gather.16.cloned.1.call-start = ((), (), s32[]{:S(2)}) async-start(), calls=%async_computation.11 | async-start | bytes 5898240 | tf_op jit(solution)/shard_map/all_gather | solution.py:159
  74.5 589.2 %all-gather.18.cloned.1.call-start = ((), (), s32[]{:S(2)}) async-start(), calls=%async_computation.12 | async-start | bytes 5898240 | tf_op jit(solution)/shard_map/all_gather | solution.py:160
  75.0 602.3 %all-gather.20.cloned.1.call-start = ((), (), s32[]{:S(2)}) async-start(), calls=%async_computation.13 | async-start | bytes 5898240 | tf_op jit(solution)/shard_map/all_gather | solution.py:161
  75.8 1422.9 %reduce-scatter.10.cloned.1.call-start = ((), (), s32[]{:S(2)}) async-start(), calls=%async_computation.14 | async-start | bytes 14155776 | tf_op jit(solution)/shard_map/reduce_scatter | solution.py:252
  686.6 35.4 %copy-start.5 = (f32[2,512,768]{2,1,0:T(8,128)}, f32[2,512,768]{2,1,0:T(8,128)S(1)}, u32[]{:S(2)}) copy-start(f32[2,512,768]{2,1,0:T(8,128)S(1)} %get-tuple-element.392) | copy-start | bytes 9437188
  686.6 35.4 %copy-start.36 = (f32[2,512]{1,0:T(2,128)}, f32[2,512]{1,0:T(2,128)S(1)}, u32[]{:S(2)}) copy-start(f32[2,512]{1,0:T(2,128)S(1)} %broadcast_multiply_fusion.5) | copy-start | bytes 12292
  1291.5 417.4 %reduce-scatter.12.cloned.1.call-start = ((), (), s32[]{:S(2)}) async-start(), calls=%async_computation.15 | async-start | bytes 14155776 | tf_op jit(solution)/shard_map/reduce_scatter | solution.py:255
  1292.2 467.1 %reduce-scatter.22.cloned.1.call-start = ((), (), s32[]{:S(2)}) async-start(), calls=%async_computation.20 | async-start | bytes 4423680
  1295.6 205.0 %copy-start.15 = (f32[2,512,12,64]{1,3,2,0:T(8,128)S(1)}, f32[2,512,12,64]{1,3,2,0:T(8,128)}, u32[]{:S(2)}) copy-start(f32[2,512,12,64]{1,3,2,0:T(8,128)} %broadcast_multiply_fusion) | copy-start | bytes 9437188
  1295.6 205.0 %copy-start.28 = (f32[2,512,32]{1,2,0:T(8,128)S(1)}, f32[2,512,32]{1,2,0:T(8,128)}, u32[]{:S(2)}) copy-start(f32[2,512,32]{1,2,0:T(8,128)} %copy-done.27) | copy-start | bytes 393220
  1295.6 205.0 %copy-start.30 = (f32[2,512,32]{1,2,0:T(8,128)S(1)}, f32[2,512,32]{1,2,0:T(8,128)}, u32[]{:S(2)}) copy-start(f32[2,512,32]{1,2,0:T(8,128)} %copy-done.29) | copy-start | bytes 393220
  1719.7 68.4 %reduce-scatter.14.cloned.1.call-start = ((), (), s32[]{:S(2)}) async-start(), calls=%async_computation.16 | async-start | bytes 1474560 | tf_op jit(solution)/shard_map/reduce_scatter | solution.py:275
  1725.4 113.1 %reduce-scatter.16.cloned.1.call-start = ((), (), s32[]{:S(2)}) async-start(), calls=%async_computation.17 | async-start | bytes 5898240 | tf_op jit(solution)/shard_map/reduce_scatter | solution.py:278
  1735.6 153.4 %reduce-scatter.18.cloned.1.call-start = ((), (), s32[]{:S(2)}) async-start(), calls=%async_computation.18 | async-start | bytes 5898240 | tf_op jit(solution)/shard_map/reduce_scatter | solution.py:281
  1746.8 192.6 %reduce-scatter.20.cloned.1.call-start = ((), (), s32[]{:S(2)}) async-start(), calls=%async_computation.19 | async-start | bytes 5898240 | tf_op jit(solution)/shard_map/reduce_scatter | solution.py:284
  1758.1 364.0 %all-reduce.14.cloned.1.call-start = ((), (), s32[]{:S(2)}) async-start(), calls=%async_computation.21 | async-start | bytes 10027008 | tf_op jit(solution)/shard_map/psum | solution.py:301
  1939.4 38.2 %copy-start.6 = (f32[2,512,768]{2,1,0:T(8,128)S(1)}, f32[2,512,768]{2,1,0:T(8,128)}, u32[]{:S(2)}) copy-start(f32[2,512,768]{2,1,0:T(8,128)} %copy-done.5) | copy-start | bytes 9437188
  1939.4 38.2 %copy-start.37 = (f32[2,512]{1,0:T(2,128)S(1)}, f32[2,512]{1,0:T(2,128)}, u32[]{:S(2)}) copy-start(f32[2,512]{1,0:T(2,128)} %copy-done.36) | copy-start | bytes 12292
  1939.4 38.2 %copy-start.39 = (f32[768]{0:T(1024)S(1)}, f32[768]{0:T(1024)}, u32[]{:S(2)}) copy-start(f32[768]{0:T(1024)} %convert_element_type.173) | copy-start | bytes 9220
  1939.4 38.2 %copy-start.41 = (f32[2,512]{1,0:T(2,128)S(1)}, f32[2,512]{1,0:T(2,128)}, u32[]{:S(2)}) copy-start(f32[2,512]{1,0:T(2,128)} %copy-done.40) | copy-start | bytes 12292
  (64 other events, 266.3 us)
Sparse Core Ops, SparseCore 0:
  9.5 33.4 all-gather.7
  54.4 176.0 all-gather.11
  233.1 174.2 all-gather.9
  408.9 15.6 all-gather.13
  425.9 37.4 all-gather.15
  464.8 37.4 all-gather.17
  503.8 37.4 all-gather.19
  1291.6 207.1 reduce-scatter.9
  1502.3 206.5 reduce-scatter.11
  1719.8 39.4 reduce-scatter.21
  1762.4 25.5 reduce-scatter.13
  1790.5 47.9 reduce-scatter.15
  1841.0 47.9 reduce-scatter.17
  1891.4 47.9 reduce-scatter.19
  1944.1 178.0 all-reduce.13
where the time goes:
time: 2150 us; the launch traced here: 2140 us
  waiting for transfers between devices  1060 us (49%)
  matrix products  775 us (36%)
  local copies, waits for them, and re-layouts  181 us (8%)
  other arithmetic  50.1 us (2%)
  blocking collectives  39.5 us (2%)
    reduce_scatter x1, waiting for transfers between devices, local(): lax.psum_scatter(k_all.astype(jnp.bfloat16), 'seq', scatter_dimension=1,...  203 us
    reduce_scatter x1, waiting for transfers between devices, local(): lax.psum_scatter(v_all.astype(jnp.bfloat16), 'seq', scatter_dimension=1,...  203 us
    all_gather x1, waiting for transfers between devices, local(): lax.all_gather(k_local, 'seq', axis=1, tiled=True)  161 us
    all_gather x1, waiting for transfers between devices, local(): lax.all_gather(v_local, 'seq', axis=1, tiled=True)  144 us
    psum x1, waiting for transfers between devices, local(): lax.psum(owned[0].astype(jnp.bfloat16), 'seq').astype(jnp.float32)  135 us
    dot_general x8, matrix products, back_step(): jnp.einsum('sqhd,skhd->shqk', g_heads, v_part, preferred_element_type=jnp...  127 us
    dot_general x8, matrix products, attend_step(): jnp.einsum('shqk,skhd->sqhd', expo.astype(jnp.bfloat16), v_part, preferre...  107 us
    dot_general x8, matrix products, back_step(): jnp.einsum('shqk,sqhd->skhd', expo.astype(jnp.bfloat16), g_heads, preferr...  93.2 us
  transfers between devices with their start and end apart: 15, of which 11 were waited for; matrix products, arithmetic and copies ran while one was open for 17% of the time, Pallas kernels for 0%

commit v1 on v0

--- a/solution.py
+++ b/solution.py
@@ -179,7 +179,9 @@
     k_local = k_heads.reshape(seq_count, row_count, model_width)
     v_local = v_heads.reshape(seq_count, row_count, model_width)
     k_full, v_full = (
-        lax.all_gather(k_local, "seq", axis=1, tiled=True),
+        jnp.concatenate(
+            lax.all_to_all(jnp.stack([k_local] * lax.axis_size("seq")), "seq", 0, 0), axis=1
+        ),
         lax.all_gather(v_local, "seq", axis=1, tiled=True),
     )
     row_total, value_sum = attend(q_heads, q_seg, k_full, v_full, segments, row_count, score_scale)

time: 2150 us -> 2280 us (1.060)
  waiting for transfers between devices: 1060 us -> 1150 us
  local copies, waits for them, and re-layouts: 181 us -> 227 us
    all_to_all x0 -> x1, waiting for transfers between devices: none -> 393 us  [local(): lax.all_to_all(jnp.stack([k_local] * lax.axis_size('seq')), 'seq', 0, 0)]
    all_gather x1, waiting for transfers between devices: 161 us -> 0.02 us  [local(): lax.all_gather(k_local, 'seq', axis=1, tiled=True)]
    all_gather x1, waiting for transfers between devices: 144 us -> 0.01 us  [local(): lax.all_gather(v_local, 'seq', axis=1, tiled=True)]
    dynamic_slice x0 -> x16, local copies, waits for them, and re-layouts: none -> 26.5 us  [attend_step(): lax.dynamic_slice_in_dim(k_full, start, block, 1)]
    dot_general x8, matrix products: 107 us -> 84.4 us  [attend_step(): jnp.einsum('shqk,skhd->sqhd', expo.astype(jnp.bfloat16), v_part, preferre...]
  transfers between devices with their start and end apart: 15 -> 16, of which waited for: 11 -> 10; matrix products, arithmetic and copies ran while one was open for 17% -> 20% of each run, Pallas kernels for 0% -> 0%
where the time goes in v1:
time: 2280 us; the launch traced here: 2270 us
  waiting for transfers between devices  1150 us (50%)
  matrix products  773 us (34%)
  local copies, waits for them, and re-layouts  227 us (10%)
  other arithmetic  49.6 us (2%)
  blocking collectives  38.9 us (2%)
    all_to_all x1, waiting for transfers between devices, local(): lax.all_to_all(jnp.stack([k_local] * lax.axis_size('seq')), 'seq', 0, 0)  393 us
    reduce_scatter x1, waiting for transfers between devices, local(): lax.psum_scatter(k_all.astype(jnp.bfloat16), 'seq', scatter_dimension=1,...  203 us
    reduce_scatter x1, waiting for transfers between devices, local(): lax.psum_scatter(v_all.astype(jnp.bfloat16), 'seq', scatter_dimension=1,...  203 us
    psum x1, waiting for transfers between devices, local(): lax.psum(owned[0].astype(jnp.bfloat16), 'seq').astype(jnp.float32)  135 us
    dot_general x8, matrix products, back_step(): jnp.einsum('sqhd,skhd->shqk', g_heads, v_part, preferred_element_type=jnp...  126 us
    dot_general x8, matrix products, attend_step(): jnp.einsum('sqhd,skhd->shqk', q_heads, k_part, preferred_element_type=jnp...  108 us
    dot_general x8, matrix products, back_step(): jnp.einsum('sqhd,skhd->shqk', q_heads, k_part, preferred_element_type=jnp...  92.3 us
    dot_general x8, matrix products, attend_step(): jnp.einsum('shqk,skhd->sqhd', expo.astype(jnp.bfloat16), v_part, preferre...  84.4 us
  transfers between devices with their start and end apart: 16, of which 10 were waited for; matrix products, arithmetic and copies ran while one was open for 20% of the time, Pallas kernels for 0%

profile of v1, /device:TPU:0, one launch (start us, length us, event | category | flops | bytes accessed | tf_op | source)
XLA Modules:
  0.0 2273.6 jit_solution(6400160967736142496)
XLA Ops:
  8.0 35.1 %all-gather.8.cloned.1.call-done = bf16[768,2304]{1,0:T(8,128)(2,1)} async-done(((bf16[192,2304]{1,0:T(8,128)(2,1)}), bf16[768,2304]{1,0:T(8,128)(2,1)}) %all-gather.8.cloned.1.call-update) | async-done | bytes 3538960 | tf_op jit(solution)/shard_map/all_gather | solution.py:157
  97.2 392.7 %all-to-all-done = bf16[8,2,512,768]{2,3,1,0:T(8,128)(2,1)} async-done(((bf16[8,2,512,768]{2,3,1,0:T(8,128)(2,1)}), bf16[8,2,512,768]{2,3,1,0:T(8,128)(2,1)}, u32[]{:S(2)}, u32[]{:S(2)}) %all-to-all-start) | async-done | bytes 12582944 | tf_op jit(solution)/shard_map/all_to_all | solution.py:183
  489.9 16.7 copy.86
  506.7 16.0 copy.89
  522.7 271.7 %while.28 = (s32[]{:T(128)}, f32[2,12,512]{2,1,0:T(8,128)S(1)}, f32[2,512,12,64]{1,3,2,0:T(8,128)}, s32[2,512]{1,0:T(2,128)S(1)}, s32[8]{0:T(128)S(1)}, /*index=...) while((s32[]{:T(128)}, f32[2,12,512]{2,1,0:T(8,128)S(1)}, ...), condition=%wide.region_2.3_spmd.clone, body=%wide.region_0.2_spmd.clone.sunk | while | flops 1650470912 | bytes 99828008 | solution.py:86
  596.3 14.2 fusion.117
  842.7 18.8 multiply_convert_fusion.1
  907.1 521.5 %while.29 = (s32[]{:T(128)}, f32[2,512,12,64]{1,3,2,0:T(8,128)}, bf16[2,4096,768]{1,2,0:T(8,128)(2,1)}, bf16[2,4096,768]{2,1,0:T(8,128)(2,1)}, s32[8]{0:T(128)S(...) while((s32[]{:T(128)}, f32[2,512,12,64]{1,3,2,0:T(8,128)}, ...), condition=%wide.region_13.14_spmd.clone, body=%wide.region_12.13_spmd.clone.sunk | while | flops 4080533504 | bytes 159449392 | solution.py:134
  924.2 15.8 fusion.129
  988.5 15.8 fusion.129
  1053.8 15.8 fusion.129
  1119.0 15.8 fusion.129
  1184.4 15.8 fusion.129
  1249.6 15.8 fusion.129
  1314.9 15.8 fusion.129
  1380.1 15.8 fusion.129
  1432.8 202.9 %reduce-scatter.10.cloned.1.call-done = bf16[2,512,768]{1,2,0:T(8,128)(2,1)} async-done(((bf16[2,4096,768]{1,2,0:T(8,128)(2,1)}), bf16[2,512,768]{1,2,0:T(8,128)(2,1)}) %reduce-scatter.10.cloned.1.call-update) | async-done | bytes 1572880 | tf_op jit(solution)/shard_map/reduce_scatter | solution.py:254
  1643.1 202.7 %reduce-scatter.12.cloned.1.call-done = bf16[2,512,768]{2,1,0:T(8,128)(2,1)} async-done(((bf16[2,4096,768]{2,1,0:T(8,128)(2,1)}), bf16[2,512,768]{2,1,0:T(8,128)(2,1)}) %reduce-scatter.12.cloned.1.call-update) | async-done | bytes 1572880 | tf_op jit(solution)/shard_map/reduce_scatter | solution.py:257
  1898.6 25.9 %reduce-scatter.14.cloned.1.call-done = bf16[192,768]{1,0:T(8,128)(2,1)} async-done(((bf16[768,768]{1,0:T(8,128)(2,1)}), bf16[192,768]{1,0:T(8,128)(2,1)}) %reduce-scatter.14.cloned.1.call-update) | async-done | bytes 294928 | tf_op jit(solution)/shard_map/reduce_scatter | solution.py:277
  1924.5 50.4 %reduce-scatter.16.cloned.1.call-done = bf16[192,3072]{1,0:T(8,128)(2,1)} async-done(((bf16[768,3072]{1,0:T(8,128)(2,1)}), bf16[192,3072]{1,0:T(8,128)(2,1)}) %reduce-scatter.16.cloned.1.call-update) | async-done | bytes 1179664 | tf_op jit(solution)/shard_map/reduce_scatter | solution.py:280
  1974.8 50.5 %reduce-scatter.18.cloned.1.call-done = bf16[192,3072]{1,0:T(8,128)(2,1)} async-done(((bf16[768,3072]{1,0:T(8,128)(2,1)}), bf16[192,3072]{1,0:T(8,128)(2,1)}) %reduce-scatter.18.cloned.1.call-update) | async-done | bytes 1179664 | tf_op jit(solution)/shard_map/reduce_scatter | solution.py:283
  2025.3 50.4 %reduce-scatter.20.cloned.1.call-done = bf16[768,768]{1,0:T(8,128)(2,1)} async-done(((bf16[3072,768]{1,0:T(8,128)(2,1)}), bf16[768,768]{1,0:T(8,128)(2,1)}) %reduce-scatter.20.cloned.1.call-update) | async-done | bytes 1179664 | tf_op jit(solution)/shard_map/reduce_scatter | solution.py:286
  2089.0 22.7 all-reduce.8
  2123.7 134.8 %all-reduce.14.cloned.1.call-done = (bf16[192,2304]{0,1:T(8,128)(2,1)}, bf16[192,768]{1,0:T(8,128)(2,1)}, bf16[192,3072]{1,0:T(8,128)(2,1)}, bf16[192,3072]{1,0:T(8,128)(2,1)}, bf16[768,768]{1,0:T(8,128)(2,1)}) async-done(((bf16[192,2304]{0,1:T(8,128)(2,1)}, bf16[192,768]{1,0:T(8,128)(2,1)}, bf16[192,3072]{1,0:T(8,128)(2,1)}, bf16[192,3072]{1,0:T(8,128)(2,1)}, bf16[768,768]{1,0:T(8,128)(2,1)}), ...) | async-done | bytes 4718608 | tf_op jit(solution)/shard_map/psum | solution.py:303
  (464 shorter events, 885.7 us)
Async XLA Ops:
  7.2 35.9 %all-gather.8.cloned.1.call-start = ((), (), s32[]{:S(2)}) async-start(), calls=%async_computation.8 | async-start | bytes 4423680 | tf_op jit(solution)/shard_map/all_gather | solution.py:157
  7.9 498.8 %all-gather.10.cloned.1.call-start = ((), (), s32[]{:S(2)}) async-start(), calls=%async_computation.9 | async-start | bytes 14155776 | tf_op jit(solution)/shard_map/all_gather | solution.py:185
  54.2 742.7 %all-gather.12.cloned.1.call-start = ((), (), s32[]{:S(2)}) async-start(), calls=%async_computation.10 | async-start | bytes 1474560 | tf_op jit(solution)/shard_map/all_gather | solution.py:158
  78.4 411.5 %all-to-all-start = ((bf16[8,2,512,768]{2,3,1,0:T(8,128)(2,1)}), bf16[8,2,512,768]{2,3,1,0:T(8,128)(2,1)}, u32[]{:S(2)}, u32[]{:S(2)}) async-start(bf16[8,2,512,768]{2,3,1,0:T(8,128)(2,1)} %stack.3), calls=%async_computation | async-start | bytes 25165824 | tf_op jit(solution)/shard_map/all_to_all | solution.py:183
  84.1 718.4 %all-gather.14.cloned.1.call-start = ((), (), s32[]{:S(2)}) async-start(), calls=%async_computation.11 | async-start | bytes 5898240 | tf_op jit(solution)/shard_map/all_gather | solution.py:159
  84.7 728.6 %all-gather.16.cloned.1.call-start = ((), (), s32[]{:S(2)}) async-start(), calls=%async_computation.12 | async-start | bytes 5898240 | tf_op jit(solution)/shard_map/all_gather | solution.py:160
  85.3 741.7 %all-gather.18.cloned.1.call-start = ((), (), s32[]{:S(2)}) async-start(), calls=%async_computation.13 | async-start | bytes 5898240 | tf_op jit(solution)/shard_map/all_gather | solution.py:161
  85.9 809.7 %all-gather.20.cloned.1.call-start = ((), (), s32[]{:S(2)}) async-start(), calls=%async_computation.14 | async-start | bytes 14155776 | tf_op jit(solution)/shard_map/all_gather | solution.py:220
  95.4 1540.3 %reduce-scatter.10.cloned.1.call-start = ((), (), s32[]{:S(2)}) async-start(), calls=%async_computation.15 | async-start | bytes 14155776 | tf_op jit(solution)/shard_map/reduce_scatter | solution.py:254
  836.3 35.5 %copy-start.5 = (f32[2,512,768]{2,1,0:T(8,128)}, f32[2,512,768]{2,1,0:T(8,128)S(1)}, u32[]{:S(2)}) copy-start(f32[2,512,768]{2,1,0:T(8,128)S(1)} %get-tuple-element.422) | copy-start | bytes 9437188
  1428.7 417.2 %reduce-scatter.12.cloned.1.call-start = ((), (), s32[]{:S(2)}) async-start(), calls=%async_computation.16 | async-start | bytes 14155776 | tf_op jit(solution)/shard_map/reduce_scatter | solution.py:257
  1429.4 466.8 %reduce-scatter.22.cloned.1.call-start = ((), (), s32[]{:S(2)}) async-start(), calls=%async_computation.21 | async-start | bytes 4423680
  1432.8 204.8 %copy-start.16 = (f32[2,512,12,64]{1,3,2,0:T(8,128)S(1)}, f32[2,512,12,64]{1,3,2,0:T(8,128)}, u32[]{:S(2)}) copy-start(f32[2,512,12,64]{1,3,2,0:T(8,128)} %broadcast_multiply_fusion) | copy-start | bytes 9437188
  1432.8 204.8 %copy-start.29 = (f32[2,512,32]{1,2,0:T(8,128)S(1)}, f32[2,512,32]{1,2,0:T(8,128)}, u32[]{:S(2)}) copy-start(f32[2,512,32]{1,2,0:T(8,128)} %copy-done.28) | copy-start | bytes 393220
  1432.8 204.8 %copy-start.31 = (f32[2,512,32]{1,2,0:T(8,128)S(1)}, f32[2,512,32]{1,2,0:T(8,128)}, u32[]{:S(2)}) copy-start(f32[2,512,32]{1,2,0:T(8,128)} %copy-done.30) | copy-start | bytes 393220
  1856.6 67.9 %reduce-scatter.14.cloned.1.call-start = ((), (), s32[]{:S(2)}) async-start(), calls=%async_computation.17 | async-start | bytes 1474560 | tf_op jit(solution)/shard_map/reduce_scatter | solution.py:277
  1862.3 112.5 %reduce-scatter.16.cloned.1.call-start = ((), (), s32[]{:S(2)}) async-start(), calls=%async_computation.18 | async-start | bytes 5898240 | tf_op jit(solution)/shard_map/reduce_scatter | solution.py:280
  1872.6 152.8 %reduce-scatter.18.cloned.1.call-start = ((), (), s32[]{:S(2)}) async-start(), calls=%async_computation.19 | async-start | bytes 5898240 | tf_op jit(solution)/shard_map/reduce_scatter | solution.py:283
  1883.7 192.0 %reduce-scatter.20.cloned.1.call-start = ((), (), s32[]{:S(2)}) async-start(), calls=%async_computation.20 | async-start | bytes 5898240 | tf_op jit(solution)/shard_map/reduce_scatter | solution.py:286
  1895.1 363.4 %all-reduce.14.cloned.1.call-start = ((), (), s32[]{:S(2)}) async-start(), calls=%async_computation.22 | async-start | bytes 10027008 | tf_op jit(solution)/shard_map/psum | solution.py:303
  2075.7 38.2 %copy-start.6 = (f32[2,512,768]{2,1,0:T(8,128)S(1)}, f32[2,512,768]{2,1,0:T(8,128)}, u32[]{:S(2)}) copy-start(f32[2,512,768]{2,1,0:T(8,128)} %copy-done.5) | copy-start | bytes 9437188
  2075.7 38.2 %copy-start.38 = (f32[2,512]{1,0:T(2,128)S(1)}, f32[2,512]{1,0:T(2,128)}, u32[]{:S(2)}) copy-start(f32[2,512]{1,0:T(2,128)} %copy-done.37) | copy-start | bytes 12292
  2075.7 38.2 %copy-start.40 = (f32[768]{0:T(1024)S(1)}, f32[768]{0:T(1024)}, u32[]{:S(2)}) copy-start(f32[768]{0:T(1024)} %convert_element_type.175) | copy-start | bytes 9220
  2075.7 38.2 %copy-start.42 = (f32[2,512]{1,0:T(2,128)S(1)}, f32[2,512]{1,0:T(2,128)}, u32[]{:S(2)}) copy-start(f32[2,512]{1,0:T(2,128)} %copy-done.41) | copy-start | bytes 12292
  (81 other events, 335.4 us)
Sparse Core Ops, SparseCore 0:
  9.5 33.4 all-gather.7
  54.4 408.8 all-gather.9
  464.9 14.6 all-gather.11
  481.0 37.4 all-gather.13
  519.9 37.4 all-gather.15
  558.7 37.4 all-gather.17
  598.8 176.1 all-gather.19
  1428.8 206.8 reduce-scatter.9
  1639.3 206.5 reduce-scatter.11
  1856.7 39.4 reduce-scatter.21
  1898.8 25.6 reduce-scatter.13
  1926.9 47.9 reduce-scatter.15
  1977.4 47.9 reduce-scatter.17
  2027.7 47.9 reduce-scatter.19
  2080.4 178.0 all-reduce.13
